TPU v7x, 32 devices: a whole 2x2x4 slice. The times are simulated.
32 devices in a mesh: parts: 2 (over y), mkt: 8 (over z, x), draw: 2 (over core).
Axes of the slice: x: 2, y: 2, z: 4, core: 2. Of those that a mesh axis runs over, the one named last changes fastest.
Arguments:
- characters: float32 [128, 6, 128], P(('parts', 'mkt')), parts along dimension 0, may hold values from -3 to 3
- taste_draws: float32 [128, 6, 4096], P(('parts', 'mkt'), None, 'draw'), parts along dimension 0, may hold values from -3 to 3
- prices: float32 [128, 128], P(('parts', 'mkt')), parts along dimension 0, may hold values from 0.5 to 2
- obs_shares: float32 [128, 128], P(('parts', 'mkt')), parts along dimension 0, may hold values from 0 to 1, as said below
- firm_ids: int32 [128, 128], P(('parts', 'mkt')), parts along dimension 0, may hold values from 0 to 7
- owner_step: int32 [128, 1], P(('parts', 'mkt')), parts along dimension 0, may hold values from 0 to 7; in each aligned block of 8 rows (0 to 7, 8 to 15, ...) at most 4 rows name the same one
- spread_coefs: float32 [6], replicated, may hold values from 0.2 to 0.6
- price_params: float32 [2], replicated, may hold values from 0 to 0.5
Outputs:
- mean_util: float32 [128, 128], P(('parts', 'mkt', 'draw')), parts along dimension 0
- markups: float32 [16, 8, 4, 128], P(('parts', 'mkt'), None, 'draw'), parts along dimension 0
There are 2 independent parts, one for each index of `parts`. A program takes and returns all parts, laid end to end along the dimension named above; an argument that names none is the same for every part. Nothing has to cross between parts.
Inputs may be any that keep to these rules, and one draw needn't show every extreme that they name: `owner_step`: among the markets of one index of mkt, no value occurs more than 4 times, and in every draw some value occurs exactly 4 times among the markets of some device. `obs_shares`: every entry is positive, and each row sums to between 2/3 and 4/5.
All inputs are finite; a program needn't handle non-finite values.
Results may differ from a plain program's by a relative error of at most 0.0003.
Values sent between devices are 32-bit elements; how exact they have to be, the bound alone decides.
A program may use at most 64 MiB of HBM per device.

v0:
```python
import jax
import jax.numpy as jnp
from jax import lax
from jax.sharding import PartitionSpec as P

ITERS = 4
CAPC = 2
W = 8


HIGH = lax.Precision.HIGHEST


def shifted(block, axis, distance):
    devices = range(lax.axis_size(axis))
    route = [((i - distance) % len(devices), i) for i in devices]
    return lax.ppermute(block, axis, route)


def utilities(characters, taste_draws, prices, spread_coefs, price_params):
    sensitivity = jnp.exp(price_params[0] + price_params[1] * taste_draws[0])
    loadings = characters * spread_coefs[:, None]
    spread = jnp.dot(loadings.T, taste_draws, precision=HIGH, preferred_element_type=jnp.float32)
    spread = spread - prices[:, None] * sensitivity[None, :]
    return (spread, sensitivity)


def purchase(mean_value, spread):
    exp_util = jnp.exp(mean_value[:, None] + spread)
    return exp_util / (1.0 + jnp.sum(exp_util, axis=0, keepdims=True))


def jacobian_of(purchase_prob, sensitivity, firm_ids, draw_count):
    own_slope = (
        jnp.dot(purchase_prob, sensitivity, precision=HIGH, preferred_element_type=jnp.float32)
        / draw_count
    )
    cross_term = (
        jnp.dot(
            purchase_prob * sensitivity[None, :],
            purchase_prob.T,
            precision=HIGH,
            preferred_element_type=jnp.float32,
        )
        / draw_count
    )
    same_firm = (firm_ids[:, None] == firm_ids[None, :]).astype(jnp.float32)
    return same_firm * (jnp.diag(own_slope) - cross_term)


def slot_ranks(offsets, per_device):
    places = jnp.arange(per_device, dtype=jnp.int32)
    earlier = places[None, :] < places[:, None]
    match = offsets[:, None] == offsets[None, :]
    return jnp.sum(jnp.logical_and(match, earlier), axis=1)


def partial_shares(
    mean_value, characters, taste_draws, prices, spread_coefs, price_params, draw_count
):

    def partial_per_market(inputs):
        market_value, market_chars, market_taste, market_prices = inputs
        spread, sensitivity = utilities(
            market_chars, market_taste, market_prices, spread_coefs, price_params
        )
        return jnp.sum(purchase(market_value, spread), axis=1) / draw_count

    return lax.map(partial_per_market, (mean_value, characters, taste_draws, prices))


def all_jacobians(
    mean_value, characters, taste_draws, prices, firm_ids, spread_coefs, price_params, draw_count
):

    def all_per_market(inputs):
        market_value, market_chars, market_taste, market_prices, market_firms = inputs
        spread, sensitivity = utilities(
            market_chars, market_taste, market_prices, spread_coefs, price_params
        )
        return jacobian_of(purchase(market_value, spread), sensitivity, market_firms, draw_count)

    return lax.map(all_per_market, (mean_value, characters, taste_draws, prices, firm_ids))


def solve_slots(blocks, right_side):
    width = blocks.shape[-1]
    system = blocks.reshape(-1, width, width)
    vectors = right_side.reshape(-1, width)
    diagonal = jnp.diagonal(system, axis1=1, axis2=2)
    live_slot = (jnp.sum(diagonal, axis=1) > 0.0).astype(jnp.float32)
    identity = jnp.eye(width, dtype=jnp.float32)
    system = system + (1.0 - live_slot)[:, None, None] * identity[None]
    factor = jnp.linalg.cholesky(system)

    def solve_one(lower_factor, vector):
        return jax.scipy.linalg.cho_solve((lower_factor, True), vector)

    return jax.vmap(solve_one)(factor, vectors).reshape(right_side.shape)


def body(
    characters, taste_draws, prices, obs_shares, firm_ids, owner_step, spread_coefs, price_params
):
    n_draw = lax.axis_size("draw")
    core_index = lax.axis_index("draw")
    markets_here = characters.shape[0]
    half_rows = markets_here // n_draw
    draw_count = taste_draws.shape[2] * n_draw
    capacity = CAPC * n_draw
    offsets = owner_step[:, 0]
    ranks = slot_ranks(offsets, markets_here)
    slot_number = offsets * capacity + ranks
    columns = jnp.arange(W * capacity, dtype=jnp.int32)
    placing = (slot_number[None, :] == columns[:, None]).astype(jnp.float32)
    start_value = jnp.log(obs_shares) - jnp.log(1.0 - jnp.sum(obs_shares, axis=1, keepdims=True))

    def own_half(array):
        return lax.dynamic_slice_in_dim(array, core_index * half_rows, half_rows, 0)

    mine_chars = own_half(characters)
    mine_prices = own_half(prices)
    mine_obs = own_half(obs_shares)
    mine_firms = own_half(firm_ids)
    mine_taste = lax.all_to_all(taste_draws, "draw", split_axis=0, concat_axis=2, tiled=True)
    mean_value = own_half(start_value)
    for turn in range(ITERS):
        shares = partial_shares(
            mean_value, mine_chars, mine_taste, mine_prices, spread_coefs, price_params, draw_count
        )
        mean_value = mean_value + jnp.log(mine_obs) - jnp.log(shares)
    jacobians = all_jacobians(
        mean_value,
        mine_chars,
        mine_taste,
        mine_prices,
        mine_firms,
        spread_coefs,
        price_params,
        draw_count,
    )
    placing_part = lax.dynamic_slice_in_dim(placing, core_index * half_rows, half_rows, 1)
    width = jacobians.shape[-1]
    buffer = jnp.einsum("sm,mjl->sjl", placing_part, jacobians, precision=HIGH).reshape(
        W, capacity, width, width
    )
    blocks = lax.psum_scatter(buffer, "draw", scatter_dimension=1, tiled=True)
    obs_slots = jnp.dot(
        placing, obs_shares, precision=HIGH, preferred_element_type=jnp.float32
    ).reshape(W, capacity, width)
    right_side = lax.dynamic_slice_in_dim(obs_slots, core_index * CAPC, CAPC, 1)
    got_blocks = [blocks[0]]
    got_sides = [right_side[0]]
    for ahead in range(1, W):
        arrived = shifted((blocks[ahead], right_side[ahead]), "mkt", ahead)
        got_blocks.append(arrived[0])
        got_sides.append(arrived[1])
    blocks = jnp.stack(got_blocks)
    right_side = jnp.stack(got_sides)
    markups = solve_slots(blocks, right_side)
    return (mean_value, markups[None])


def solution(mesh):
    placed = (
        P(("parts", "mkt"), None, None),
        P(("parts", "mkt"), None, "draw"),
        P(("parts", "mkt"), None),
        P(("parts", "mkt"), None),
        P(("parts", "mkt"), None),
        P(("parts", "mkt"), None),
        P(),
        P(),
    )
    return jax.shard_map(
        body,
        mesh=mesh,
        in_specs=placed,
        out_specs=(P(("parts", "mkt", "draw"), None), P(("parts", "mkt"), None, "draw", None)),
        check_vma=False,
    )
```

profile of v0, /device:TPU:0, one launch (start us, length us, event | category | flops | bytes accessed | tf_op | source)
XLA Modules:
  0.0 545.4 jit_solution(619063527034756499)
XLA Ops:
  9.2 3.6 all-to-all-start
  15.6 18.8 %while.50 = (s32[]{:T(128)}, f32[4,128]{1,0:T(4,128)S(1)}, f32[4,128]{1,0:T(4,128)S(1)}, f32[4,6,128]{2,1,0:T(8,128)S(1)}, f32[6]{0:T(128)S(1)}, /*index=5*/f32[...) while((s32[]{:T(128)}, f32[4,128]{1,0:T(4,128)S(1)}, ...), condition=%wide.region_4.5_spmd, body=%wide.region_1.4_spmd.sunk | while | flops 40903424 | bytes 4451465 | solution.py:69
  17.5 2.5 fusion.141
  22.2 2.5 fusion.141
  26.9 2.5 fusion.141
  31.6 2.5 fusion.141
  34.5 18.8 %while.51 = (s32[]{:T(128)}, f32[4,128]{1,0:T(4,128)S(1)}, f32[4,128]{1,0:T(4,128)S(1)}, f32[4,6,128]{2,1,0:T(8,128)S(1)}, f32[6]{0:T(128)S(1)}, /*index=5*/f32[...) while((s32[]{:T(128)}, f32[4,128]{1,0:T(4,128)S(1)}, ...), condition=%wide.region_8.9_spmd, body=%wide.region_5.8_spmd.sunk | while | flops 40903424 | bytes 4451465 | solution.py:69
  36.4 2.5 fusion.145
  41.1 2.5 fusion.145
  45.8 2.5 fusion.145
  50.5 2.5 fusion.145
  53.3 18.8 %while.52 = (s32[]{:T(128)}, f32[4,128]{1,0:T(4,128)S(1)}, f32[4,128]{1,0:T(4,128)S(1)}, f32[4,6,128]{2,1,0:T(8,128)S(1)}, f32[6]{0:T(128)S(1)}, /*index=5*/f32[...) while((s32[]{:T(128)}, f32[4,128]{1,0:T(4,128)S(1)}, ...), condition=%wide.region_12.13_spmd, body=%wide.region_9.12_spmd.sunk | while | flops 40903424 | bytes 4451465 | solution.py:69
  55.2 2.5 fusion.149
  59.9 2.5 fusion.149
  64.6 2.5 fusion.149
  69.3 2.5 fusion.149
  72.2 18.8 %while.53 = (s32[]{:T(128)}, f32[4,128]{1,0:T(4,128)S(1)}, f32[4,128]{1,0:T(4,128)S(1)}, f32[4,6,128]{2,1,0:T(8,128)S(1)}, f32[6]{0:T(128)S(1)}, /*index=5*/f32[...) while((s32[]{:T(128)}, f32[4,128]{1,0:T(4,128)S(1)}, ...), condition=%wide.region_16.17_spmd, body=%wide.region_13.16_spmd.sunk | while | flops 40903424 | bytes 4451465 | solution.py:69
  74.1 2.5 fusion.153
  78.8 2.5 fusion.153
  83.5 2.5 fusion.153
  88.2 2.5 fusion.153
  91.0 39.6 %while.54 = (s32[]{:T(128)}, f32[4,128,128]{2,0,1:T(4,128)S(1)}, s32[4,128]{1,0:T(4,128)S(1)}, f32[4,128]{1,0:T(4,128)S(1)}, f32[4,6,128]{2,1,0:T(8,128)S(1)}, /...) while((s32[]{:T(128)}, f32[4,128,128]{2,0,1:T(4,128)S(1)}, ...), condition=%wide.region_20.21_spmd, body=%wide.region_18.20_spmd.sunk | while | flops 853648256 | bytes 6794389 | solution.py:83
  93.3 2.5 fusion.159
  103.1 2.5 fusion.159
  134.2 3.0 collective-permute-start.7
  138.8 2.6 collective-permute-start.9
  142.6 2.6 collective-permute-start.11
  150.3 7.8 %all-reduce.3.cloned.1.call-done = f32[8,4,128,128]{2,3,1,0:T(8,128)} async-done(((f32[8,4,128,128]{2,3,1,0:T(8,128)}), f32[8,4,128,128]{2,3,1,0:T(8,128)}) %all-reduce.3.cloned.1.call-update) | async-done | bytes 2097168
  172.8 6.6 %collective-permute-done.2 = f32[2,128,128]{1,2,0:T(8,128)S(1)} collective-permute-done((f32[2,128,128]{1,2,0:T(8,128)S(1)}, f32[2,128,128]{1,2,0:T(8,128)S(1)}, u32[]{:S(2)}, u32[]{:S(2)}) %collective-permute-start.2) | collective-permute-done | bytes 131104 | tf_op jit(solution)/shard_map/ppermute | solution.py:17
  179.9 7.7 %copy.52 = f32[16,128,128]{0,2,1:T(8,128)} copy(f32[16,128,128]{1,2,0:T(8,128)S(1)} %bitcast.296) | data formatting | bytes 2097152 | tf_op jit(solution)/shard_map/reshape | solution.py:88
  190.1 187.5 %custom-call.11 = f32[16,128,128]{2,1,0:T(8,128)S(1)} custom-call(f32[16,128,128]{2,1,0:T(8,128)S(1)} %fusion.83), custom_call_target="Cholesky" | custom-call | tf_op jit(solution)/shard_map/jit(cholesky)/cholesky | solution.py:94
  378.1 157.2 %custom-call.12 = f32[16,1,128,128]{2,3,1,0:T(8,128)S(1)} custom-call(f32[16,1,128,128]{3,2,1,0:T(8,128)S(1)} %select_bitcast_fusion), custom_call_target="InvertDiagBlocksLowerTriangular" | custom-call | tf_op jit(solution)/shard_map/vmap(jit(_cho_solve))/triangular_solve | solution.py:97
  (250 shorter events, 105.8 us)
Async XLA Ops:
  7.2 7.3 %copy-start = (f32[8,6,128]{2,0,1:T(8,128)S(1)}, f32[8,6,128]{2,0,1:T(8,128)}, u32[]{:S(2)}) copy-start(f32[8,6,128]{2,0,1:T(8,128)} %param.18) | copy-start | bytes 73732
  9.2 6.3 %copy-start.4 = (f32[8,128]{1,0:T(8,128)S(1)}, f32[8,128]{1,0:T(8,128)}, u32[]{:S(2)}) copy-start(f32[8,128]{1,0:T(8,128)} %param.20) | copy-start | bytes 12292
  9.2 6.4 %copy-start.1 = (f32[2]{0:T(128)S(1)}, f32[2]{0:T(128)}, u32[]{:S(2)}) copy-start(f32[2]{0:T(128)} %param.25) | copy-start | bytes 28
  9.2 6.4 %copy-start.6 = (f32[6]{0:T(128)S(1)}, f32[6]{0:T(128)}, u32[]{:S(2)}) copy-start(f32[6]{0:T(128)} %param.24) | copy-start | bytes 76
  9.2 5.4 all-to-all-start
  12.8 145.2 %all-reduce.3.cloned.1.call-start = ((), (), s32[]{:S(2)}) async-start(), calls=%async_computation.1 | async-start | bytes 4194304
  15.6 18.8 %copy-start.2 = (f32[8,128]{1,0:T(8,128)S(1)}, f32[8,128]{1,0:T(8,128)}, u32[]{:S(2)}) copy-start(f32[8,128]{1,0:T(8,128)} %param.21) | copy-start | bytes 12292
  72.2 18.8 %copy-start.5 = (s32[8,128]{1,0:T(8,128)S(1)}, s32[8,128]{1,0:T(8,128)}, u32[]{:S(2)}) copy-start(s32[8,128]{1,0:T(8,128)} %param.22) | copy-start | bytes 12292
  91.0 39.6 %copy-start.7 = (s32[8,1]{0,1:T(1,128)S(1)}, s32[8,1]{0,1:T(1,128)}, u32[]{:S(2)}) copy-start(s32[8,1]{0,1:T(1,128)} %param.23) | copy-start | bytes 100
  130.6 3.3 copy-start.3
  133.9 11.5 %copy-start.8 = (u32[32]{0:T(128)S(1)}, u32[32]{0:T(128)}, u32[]{:S(2)}) copy-start(u32[32]{0:T(128)} %constant.194) | copy-start | bytes 388
  134.2 12.4 %collective-permute-start.7 = (f32[2,128]{1,0:T(2,128)S(1)}, f32[2,128]{1,0:T(2,128)S(1)}, u32[]{:S(2)}, u32[]{:S(2)}) collective-permute-start(f32[2,128]{1,0:T(2,128)S(1)} %get-tuple-element.471), channel_id=1, source_target_pairs={{14,0},{0,2},{2,4},{4,6},{6,8},{8,10},{10,12},{12,14},{15,1},{1,3}... | collective-permute-start | bytes 3080 | tf_op jit(solution)/shard_map/ppermute | solution.py:17
  137.2 10.8 %collective-permute-start.8 = (f32[2,128]{1,0:T(2,128)S(1)}, f32[2,128]{1,0:T(2,128)S(1)}, u32[]{:S(2)}, u32[]{:S(2)}) collective-permute-start(f32[2,128]{1,0:T(2,128)S(1)} %get-tuple-element.470), channel_id=1, source_target_pairs={{12,0},{14,2},{0,4},{2,6},{4,8},{6,10},{8,12},{10,14},{13,1},{15,3... | collective-permute-start | bytes 3080 | tf_op jit(solution)/shard_map/ppermute | solution.py:17
  138.8 10.7 %collective-permute-start.9 = (f32[2,128]{1,0:T(2,128)S(1)}, f32[2,128]{1,0:T(2,128)S(1)}, u32[]{:S(2)}, u32[]{:S(2)}) collective-permute-start(f32[2,128]{1,0:T(2,128)S(1)} %get-tuple-element.469), channel_id=1, source_target_pairs={{10,0},{12,2},{14,4},{0,6},{2,8},{4,10},{6,12},{8,14},{11,1},{13,3... | collective-permute-start | bytes 3080 | tf_op jit(solution)/shard_map/ppermute | solution.py:17
  141.4 8.2 %collective-permute-start.10 = (f32[2,128]{1,0:T(2,128)S(1)}, f32[2,128]{1,0:T(2,128)S(1)}, u32[]{:S(2)}, u32[]{:S(2)}) collective-permute-start(f32[2,128]{1,0:T(2,128)S(1)} %get-tuple-element.468), channel_id=1, source_target_pairs={{8,0},{10,2},{12,4},{14,6},{0,8},{2,10},{4,12},{6,14},{9,1},{11,3}... | collective-permute-start | bytes 3080 | tf_op jit(solution)/shard_map/ppermute | solution.py:17
  142.6 7.0 %collective-permute-start.11 = (f32[2,128]{1,0:T(2,128)S(1)}, f32[2,128]{1,0:T(2,128)S(1)}, u32[]{:S(2)}, u32[]{:S(2)}) collective-permute-start(f32[2,128]{1,0:T(2,128)S(1)} %get-tuple-element.467), channel_id=1, source_target_pairs={{6,0},{8,2},{10,4},{12,6},{14,8},{0,10},{2,12},{4,14},{7,1},{9,3},... | collective-permute-start | bytes 3080 | tf_op jit(solution)/shard_map/ppermute | solution.py:17
  146.6 3.6 collective-permute-start.12
  148.1 13.2 %collective-permute-start.13 = (f32[2,128]{1,0:T(2,128)S(1)}, f32[2,128]{1,0:T(2,128)S(1)}, u32[]{:S(2)}, u32[]{:S(2)}) collective-permute-start(f32[2,128]{1,0:T(2,128)S(1)} %get-tuple-element.465), channel_id=1, source_target_pairs={{2,0},{4,2},{6,4},{8,6},{10,8},{12,10},{14,12},{0,14},{3,1},{5,3},... | collective-permute-start | bytes 3080 | tf_op jit(solution)/shard_map/ppermute | solution.py:17
  159.5 9.5 %collective-permute-start = (f32[2,128,128]{1,2,0:T(8,128)S(1)}, f32[2,128,128]{1,2,0:T(8,128)S(1)}, u32[]{:S(2)}, u32[]{:S(2)}) collective-permute-start(f32[2,128,128]{1,2,0:T(8,128)S(1)} %get-tuple-element.463), channel_id=1, source_target_pairs={{14,0},{0,2},{2,4},{4,6},{6,8},{8,10},{10,12},{12,14},{15,1},{1,3}... | collective-permute-start | bytes 393224 | tf_op jit(solution)/shard_map/ppermute | solution.py:17
  161.3 9.2 %collective-permute-start.1 = (f32[2,128,128]{1,2,0:T(8,128)S(1)}, f32[2,128,128]{1,2,0:T(8,128)S(1)}, u32[]{:S(2)}, u32[]{:S(2)}) collective-permute-start(f32[2,128,128]{1,2,0:T(8,128)S(1)} %get-tuple-element.462), channel_id=1, source_target_pairs={{12,0},{14,2},{0,4},{2,6},{4,8},{6,10},{8,12},{10,14},{13,1},{15,3... | collective-permute-start | bytes 393224 | tf_op jit(solution)/shard_map/ppermute | solution.py:17
  162.8 16.6 %collective-permute-start.2 = (f32[2,128,128]{1,2,0:T(8,128)S(1)}, f32[2,128,128]{1,2,0:T(8,128)S(1)}, u32[]{:S(2)}, u32[]{:S(2)}) collective-permute-start(f32[2,128,128]{1,2,0:T(8,128)S(1)} %get-tuple-element.461), channel_id=1, source_target_pairs={{10,0},{12,2},{14,4},{0,6},{2,8},{4,10},{6,12},{8,14},{11,1},{13,3... | collective-permute-start | bytes 393224 | tf_op jit(solution)/shard_map/ppermute | solution.py:17
  165.2 14.6 %collective-permute-start.3 = (f32[2,128,128]{1,2,0:T(8,128)S(1)}, f32[2,128,128]{1,2,0:T(8,128)S(1)}, u32[]{:S(2)}, u32[]{:S(2)}) collective-permute-start(f32[2,128,128]{1,2,0:T(8,128)S(1)} %get-tuple-element.460), channel_id=1, source_target_pairs={{8,0},{10,2},{12,4},{14,6},{0,8},{2,10},{4,12},{6,14},{9,1},{11,3}... | collective-permute-start | bytes 393224 | tf_op jit(solution)/shard_map/ppermute | solution.py:17
  166.6 13.2 %collective-permute-start.4 = (f32[2,128,128]{1,2,0:T(8,128)S(1)}, f32[2,128,128]{1,2,0:T(8,128)S(1)}, u32[]{:S(2)}, u32[]{:S(2)}) collective-permute-start(f32[2,128,128]{1,2,0:T(8,128)S(1)} %get-tuple-element.459), channel_id=1, source_target_pairs={{6,0},{8,2},{10,4},{12,6},{14,8},{0,10},{2,12},{4,14},{7,1},{9,3},... | collective-permute-start | bytes 393224 | tf_op jit(solution)/shard_map/ppermute | solution.py:17
  169.0 10.9 %collective-permute-start.5 = (f32[2,128,128]{1,2,0:T(8,128)S(1)}, f32[2,128,128]{1,2,0:T(8,128)S(1)}, u32[]{:S(2)}, u32[]{:S(2)}) collective-permute-start(f32[2,128,128]{1,2,0:T(8,128)S(1)} %get-tuple-element.458), channel_id=1, source_target_pairs={{4,0},{6,2},{8,4},{10,6},{12,8},{14,10},{0,12},{2,14},{5,1},{7,3},... | collective-permute-start | bytes 393224 | tf_op jit(solution)/shard_map/ppermute | solution.py:17
  170.5 9.4 %collective-permute-start.6 = (f32[2,128,128]{1,2,0:T(8,128)S(1)}, f32[2,128,128]{1,2,0:T(8,128)S(1)}, u32[]{:S(2)}, u32[]{:S(2)}) collective-permute-start(f32[2,128,128]{1,2,0:T(8,128)S(1)} %get-tuple-element.457), channel_id=1, source_target_pairs={{2,0},{4,2},{6,4},{8,6},{10,8},{12,10},{14,12},{0,14},{3,1},{5,3},... | collective-permute-start | bytes 393224 | tf_op jit(solution)/shard_map/ppermute | solution.py:17
Sparse Core Ops, SparseCore 0:
  134.0 24.0 all-reduce.2
where the time goes:
time: 552 us; the launch traced here: 545 us
  other arithmetic  377 us (68%)
  matrix products  69.5 us (13%)
  local copies, waits for them, and re-layouts  35.9 us (7%)
  starting transfers between devices  30.7 us (6%)
  waiting for transfers between devices  15.7 us (3%)
  between operations  15.2 us (3%)
    another operation x4, other arithmetic, solve_slots(): factor = jnp.linalg.cholesky(system)  188 us
    another operation x3, other arithmetic, solve_one(): return jax.scipy.linalg.cho_solve((lower_factor, True), vector)  157 us
    dot_general x20, matrix products, utilities(): jnp.dot(loadings.T, taste_draws, precision=HIGH, preferred_element_type=j...  49.8 us
    ppermute x14, starting transfers between devices, shifted(): return lax.ppermute(block, axis, route)  27.1 us
    exp x20, other arithmetic, utilities(): sensitivity = jnp.exp(price_params[0] + price_params[1] * taste_draws[0])  25.9 us
    slice x20, local copies, waits for them, and re-layouts, utilities(): sensitivity = jnp.exp(price_params[0] + price_params[1] * taste_draws[0])  12.2 us
  transfers between devices with their start and end apart: 16, of which 5 were waited for; matrix products, arithmetic and copies ran while one was open for 1% of the time, Pallas kernels for 0%

commit v1 on v0

v1 whole, which is shorter than its diff:
```python
import functools

import jax
import jax.numpy as jnp
from jax import lax
from jax.experimental import pallas as pl
from jax.experimental.pallas import tpu as pltpu
from jax.sharding import PartitionSpec as P

ITERS = 4
CAPC = 2
W = 8
LOG2E = 1.4426950408889634
LN2 = 0.6931471805599453
SWEEPS = 6
DOUBLINGS = 26
TOL = 3e-7
MESH = pl.DeviceIdType.MESH
HIGH = lax.Precision.HIGHEST
F32 = jnp.float32
BF16 = jnp.bfloat16


def exchange_kernel(taste_ref, out_ref, send_sem, recv_sem):
    core = lax.axis_index("draw")
    half = out_ref.shape[0]
    barrier = pltpu.get_barrier_semaphore()
    pl.semaphore_signal(barrier, inc=1, device_id={"draw": 1 - core}, device_id_type=MESH)
    pl.semaphore_wait(barrier, 1)
    copy = pltpu.make_async_remote_copy(
        src_ref=taste_ref.at[pl.ds((1 - core) * half, half)],
        dst_ref=out_ref,
        send_sem=send_sem,
        recv_sem=recv_sem,
        device_id={"draw": 1 - core},
        device_id_type=MESH,
    )
    copy.start()
    copy.wait()


def exchange(taste_draws):
    half = taste_draws.shape[0] // 2
    return pl.pallas_call(
        exchange_kernel,
        out_shape=jax.ShapeDtypeStruct((half,) + taste_draws.shape[1:], F32),
        in_specs=[pl.BlockSpec(memory_space=pl.ANY)],
        out_specs=pl.BlockSpec(memory_space=pl.ANY),
        scratch_shapes=[pltpu.SemaphoreType.DMA, pltpu.SemaphoreType.DMA],
        compiler_params=pltpu.CompilerParams(collective_id=0, has_side_effects=True),
        name="exchange",
    )(taste_draws)


def split3(value):
    high = value.astype(BF16).astype(F32)
    rest = value - high
    middle = rest.astype(BF16).astype(F32)
    return high, middle, rest - middle


def market_kernel(
    coef_ref, params_ref, steps_ref, chars_ref, taste_ref, other_ref, prices_ref, obs_ref,
    firms_ref, util_ref, placed_ref,
    e_ref, q_ref, left_ref, right_ref, stack_ref, root_ref, v_ref, n_ref, m_ref,
):
    core = lax.axis_index("draw")
    here, terms, width = chars_ref.shape
    half = here // 2
    part = taste_ref.shape[2]
    total = 2 * part
    lanes = 128
    chunks = total // lanes
    first = core * half

    row_i = lax.broadcasted_iota(jnp.int32, (width, width), 0)
    col_i = lax.broadcasted_iota(jnp.int32, (width, width), 1)
    eye = (row_i == col_i).astype(F32)

    obs_rows = [obs_ref[pl.ds(first + i, 1), :] for i in range(half)]
    firm_rows = [firms_ref[pl.ds(first + i, 1), :].astype(F32) for i in range(half)]
    rows = jnp.zeros((width, width), F32)
    for i in range(half):
        rows = jnp.where(row_i == i, obs_rows[i], rows)
        rows = jnp.where(row_i == half + i, firm_rows[i], rows)
    cols = rows.T

    finals = jnp.zeros((width, width), F32)
    for i in range(half):
        obs_row = obs_rows[i]
        obs_col = cols[:, i:i + 1]
        left_ref[...] = jnp.zeros_like(left_ref)
        for k in range(terms):
            left_ref[k:k + 1, :] = chars_ref[first + i, k:k + 1, :] * coef_ref[k] * LOG2E
        left_ref[terms:terms + 1, :] = prices_ref[pl.ds(first + i, 1), :] * (-LOG2E)
        lh, lm, ll = split3(left_ref[...])
        left = jnp.concatenate([lh, lh, lm, lm, lh, ll], axis=0).T.astype(BF16)
        right_ref[...] = jnp.zeros_like(right_ref)
        for h in range(2):
            taste = taste_ref[first + i] if h == 0 else other_ref[i]
            log_sens = (params_ref[0] + params_ref[1] * taste[0:1, :]) * LOG2E
            right_ref[0:terms, h * part:(h + 1) * part] = taste
            right_ref[terms:terms + 1, h * part:(h + 1) * part] = jnp.exp2(log_sens)
            root_ref[0:1, h * part:(h + 1) * part] = jnp.exp2(0.5 * log_sens)
        xh, xm, xl = split3(right_ref[...])
        stack_ref[...] = jnp.concatenate([xh, xm, xh, xm, xl, xh], axis=0).astype(BF16)

        wide = 4 * lanes

        def spread_chunk(c, top):
            at = pl.ds(pl.multiple_of(c * wide, wide), wide)
            s = jnp.dot(left, stack_ref[:, at], preferred_element_type=F32)
            e_ref[i, :, at] = s
            for b in range(4):
                top = jnp.maximum(top, s[:, b * lanes:(b + 1) * lanes])
            return top

        top = lax.fori_loop(
            0, total // wide, spread_chunk, jnp.full((width, lanes), -jnp.inf, F32), unroll=2
        )
        top = jnp.max(top, axis=1, keepdims=True)
        outside = 1.0 - jnp.sum(obs_row, axis=1, keepdims=True)
        start = (jnp.log(obs_col) - jnp.log(outside)) * LOG2E + top
        v_ref[...] = jnp.broadcast_to(jnp.exp2(start), (width, lanes))
        m_ref[...] = jnp.broadcast_to(top, (width, lanes))

        def first_chunk(c, acc):
            at = pl.ds(pl.multiple_of(c * lanes, lanes), lanes)
            e = jnp.exp2(e_ref[i, :, at] - m_ref[...])
            e_ref[i, :, at] = e
            inv = 1.0 / (1.0 + jnp.sum(e * v_ref[...], axis=0, keepdims=True))
            return acc + e * inv

        def next_chunk(c, acc):
            at = pl.ds(pl.multiple_of(c * lanes, lanes), lanes)
            e = e_ref[i, :, at]
            inv = 1.0 / (1.0 + jnp.sum(e * v_ref[...], axis=0, keepdims=True))
            return acc + e * inv

        for turn in range(ITERS):
            acc = lax.fori_loop(
                0, chunks, first_chunk if turn == 0 else next_chunk,
                jnp.zeros((width, lanes), F32), unroll=4,
            )
            share = jnp.sum(acc, axis=1, keepdims=True) * (1.0 / total)
            v_ref[...] = jnp.broadcast_to(obs_col / share, (width, lanes))
        mean = jnp.log(obs_col) - jnp.log(share) - top * LN2
        finals = jnp.where(col_i == i, mean, finals)

        def last_chunk(c, acc):
            at = pl.ds(pl.multiple_of(c * lanes, lanes), lanes)
            ve = e_ref[i, :, at] * v_ref[...]
            inv = 1.0 / (1.0 + jnp.sum(ve, axis=0, keepdims=True))
            root = root_ref[0:1, at]
            q = ve * (inv * root)
            high = q.astype(BF16)
            q_ref[0:width, at] = high
            q_ref[width:2 * width, at] = (q - high.astype(F32)).astype(BF16)
            return acc + q * root

        own = lax.fori_loop(0, chunks, last_chunk, jnp.zeros((width, lanes), F32), unroll=4)
        own = jnp.sum(own, axis=1, keepdims=True)
        both = lax.dot_general(
            q_ref[...], q_ref[...], (((1,), (1,)), ((), ())), preferred_element_type=F32
        )
        cross = both[0:width, 0:width] + (both[0:width, width:] + both[width:, 0:width])
        same = cols[:, half + i:half + i + 1] == firm_rows[i]
        n_ref[i] = jnp.where(same, eye * own - cross, 0.0) * (1.0 / total)

    util_ref[...] = finals.T[0:half, :]

    scales, c_rows, c_cols, y_rows, y_cols = [], [], [], [], []
    for i in range(half):
        jac = n_ref[i]
        diag = jac * eye
        s_row = lax.rsqrt(jnp.sum(diag, axis=0, keepdims=True))
        s_col = lax.rsqrt(jnp.sum(diag, axis=1, keepdims=True))
        n_ref[i] = eye - s_col * jac * s_row
        scales.append(s_row)
        c_rows.append(s_row * obs_rows[i])
        c_cols.append(s_col * cols[:, i:i + 1])
    y_rows = tuple(c_rows)

    def sweep(_, ys):
        out = []
        for i in range(half):
            y_col = c_cols[i] + jnp.sum(n_ref[i] * ys[i], axis=1, keepdims=True)
            out.append(c_rows[i] + jnp.sum(n_ref[i] * y_col, axis=0, keepdims=True))
        return tuple(out)

    y_rows = lax.fori_loop(0, SWEEPS, sweep, y_rows)
    rests = []
    for i in range(half):
        n_col = jnp.sum(n_ref[i] * y_rows[i], axis=1, keepdims=True)
        n_row = jnp.sum(eye * n_col, axis=0, keepdims=True)
        rests.append(c_rows[i] + n_row - y_rows[i])

    def size_of(vectors, against):
        worst = jnp.zeros((1, 1), F32)
        for i in range(half):
            top = jnp.max(jnp.abs(vectors[i]), axis=1, keepdims=True)
            worst = jnp.maximum(worst, top / jnp.max(jnp.abs(against[i]), axis=1, keepdims=True))
        return jnp.max(worst)

    def again(state):
        return jnp.logical_and(state[0] < DOUBLINGS, state[1] > TOL)

    def double(state):
        step, _, errors = state
        added, fresh = [], []
        for i in range(half):
            power = n_ref[i]
            eight = jnp.broadcast_to(errors[i], (8, width))
            more = jnp.dot(eight, power, precision=HIGH, preferred_element_type=F32)[0:1, :]
            added.append(more)
            fresh.append(errors[i] + more)
            n_ref[i] = jnp.dot(power, power, precision=HIGH, preferred_element_type=F32)
        return step + 1, size_of(added, y_rows), tuple(fresh)

    state = lax.while_loop(again, double, (0, size_of(rests, y_rows), tuple(rests)))
    out_row = lax.broadcasted_iota(jnp.int32, placed_ref.shape, 0)
    placed = jnp.zeros(placed_ref.shape, F32)
    for i in range(half):
        x = scales[i] * (y_rows[i] + state[2][i])
        mine = steps_ref[first + i]
        rank = 0
        for other in range(here):
            hit = jnp.logical_and(steps_ref[other] == mine, other < first + i)
            rank = rank + hit.astype(jnp.int32)
        upper = (rank >= CAPC).astype(jnp.int32)
        at = upper * (W * CAPC) + mine * CAPC + (rank - upper * CAPC)
        placed = jnp.where(out_row == at, x, placed)
    placed_ref[...] = placed


def solve_markets(coefs, params, steps, chars, taste, other, prices, obs, firms):
    here, terms, width = chars.shape
    half = here // 2
    total = 2 * taste.shape[2]
    smem = pl.BlockSpec(memory_space=pltpu.SMEM)
    vmem = pl.BlockSpec(memory_space=pltpu.VMEM)
    padded = -(-(terms + 1) // 8) * 8
    return pl.pallas_call(
        market_kernel,
        out_shape=(
            jax.ShapeDtypeStruct((half, width), F32),
            jax.ShapeDtypeStruct((2 * W * CAPC, width), F32),
        ),
        in_specs=[smem] * 3 + [vmem] * 6,
        out_specs=(vmem, vmem),
        scratch_shapes=[
            pltpu.VMEM((half, width, total), F32),
            pltpu.VMEM((2 * width, total), BF16),
            pltpu.VMEM((padded, width), F32),
            pltpu.VMEM((padded, total), F32),
            pltpu.VMEM((6 * padded, total), BF16),
            pltpu.VMEM((8, total), F32),
            pltpu.VMEM((width, 128), F32),
            pltpu.VMEM((half, width, width), F32),
            pltpu.VMEM((width, 128), F32),
        ],
        name="markets",
    )(coefs, params, steps, chars, taste, other, prices, obs, firms)


def route_kernel(markets, placed_ref, out_ref, got_ref, send_sem, recv_sem):
    core = lax.axis_index("draw")
    me = lax.axis_index("mkt")
    pairs = [(w, flip) for w in range(W) for flip in range(2) if (w, flip) != (0, 0)]
    barrier = pltpu.get_barrier_semaphore()

    def peer(step, flip):
        to_core = core if flip == 0 else 1 - core
        return {"mkt": lax.rem(me + step + markets, markets), "draw": to_core}

    for w, flip in pairs:
        pl.semaphore_signal(barrier, inc=1, device_id=peer(-w, flip), device_id_type=MESH)
    pl.semaphore_wait(barrier, len(pairs))
    copies = []
    for w, flip in pairs:
        to_core = core if flip == 0 else 1 - core
        copy = pltpu.make_async_remote_copy(
            src_ref=placed_ref.at[to_core, w],
            dst_ref=got_ref.at[flip, w],
            send_sem=send_sem.at[flip, w],
            recv_sem=recv_sem.at[flip, w],
            device_id=peer(w, flip),
            device_id_type=MESH,
        )
        copy.start()
        copies.append(copy)
    for copy in copies:
        copy.wait()
    out_ref[0, 0] = placed_ref[core, 0] + got_ref[1, 0]
    for w in range(1, W):
        out_ref[0, w] = got_ref[0, w] + got_ref[1, w]


def route(markets, placed):
    width = placed.shape[-1]
    vmem = pl.BlockSpec(memory_space=pltpu.VMEM)
    return pl.pallas_call(
        functools.partial(route_kernel, markets),
        out_shape=jax.ShapeDtypeStruct((1, W, CAPC, width), F32),
        in_specs=[vmem],
        out_specs=vmem,
        scratch_shapes=[
            pltpu.VMEM((2, W, CAPC, width), F32),
            pltpu.SemaphoreType.DMA((2, W)),
            pltpu.SemaphoreType.DMA((2, W)),
        ],
        compiler_params=pltpu.CompilerParams(collective_id=1, has_side_effects=True),
        name="route",
    )(placed.reshape(2, W, CAPC, width))


def body(
    markets,
    characters, taste_draws, prices, obs_shares, firm_ids, owner_step, spread_coefs, price_params,
):
    other = exchange(taste_draws)
    mean_util, placed = solve_markets(
        spread_coefs, price_params, owner_step[:, 0], characters, taste_draws, other,
        prices, obs_shares, firm_ids,
    )
    return mean_util, route(markets, placed)


def solution(mesh):
    placed = (
        P(("parts", "mkt"), None, None),
        P(("parts", "mkt"), None, "draw"),
        P(("parts", "mkt"), None),
        P(("parts", "mkt"), None),
        P(("parts", "mkt"), None),
        P(("parts", "mkt"), None),
        P(),
        P(),
    )
    return jax.shard_map(
        functools.partial(body, mesh.shape["mkt"]),
        mesh=mesh,
        in_specs=placed,
        out_specs=(P(("parts", "mkt", "draw"), None), P(("parts", "mkt"), None, "draw", None)),
        check_vma=False,
    )
```

time: 552 us -> 47.9 us (0.09); the launches traced: 545 us -> 47.6 us
  other arithmetic: 377 us -> 0 us
  matrix products: 69.5 us -> 0 us
  Pallas kernels: 0 us -> 42.2 us
  local copies, waits for them, and re-layouts: 35.9 us -> 4.67 us
  starting transfers between devices: 30.7 us -> 0 us
  waiting for transfers between devices: 15.7 us -> 0 us
  between operations: 15.2 us -> 0.65 us
    another operation x7 -> x0, other arithmetic: 345 us -> none  [the longest x4 188 us: solve_slots(): factor = jnp.linalg.cholesky(system)]
    dot_general x30 -> x0, matrix products: 66.1 us -> none  [the longest x20 49.8 us: utilities(): jnp.dot(loadings.T, taste_draws, precision=HIGH, preferred_element_type=j...]
    pallas_call x0 -> x3, Pallas kernels: none -> 42.2 us  [the longest x1 30.6 us: solve_markets(): pl.pallas_call(market_kernel, out_shape=(jax.ShapeDtypeStruct((half, widt...]
    ppermute x14 -> x0, starting transfers between devices: 27.1 us -> none  [shifted(): return lax.ppermute(block, axis, route)]
    exp x20 -> x0, other arithmetic: 25.9 us -> none  [utilities(): sensitivity = jnp.exp(price_params[0] + price_params[1] * taste_draws[0])]
    slice x20 -> x0, local copies, waits for them, and re-layouts: 12.2 us -> none  [utilities(): sensitivity = jnp.exp(price_params[0] + price_params[1] * taste_draws[0])]
    reshape x2 -> x0, local copies, waits for them, and re-layouts: 9.59 us -> none  [the longest x1 7.69 us: solve_slots(): system = blocks.reshape(-1, width, width)]
    unnamed x2 -> x0, waiting for transfers between devices: 7.85 us -> none
  transfers between devices with their start and end apart: 16 -> 0, of which waited for: 5 -> 0; matrix products, arithmetic and copies ran while one was open for 1% -> 0% of each run, Pallas kernels for 0% -> 0%
where the time goes in v1:
time: 47.9 us; the launch traced here: 47.6 us
  Pallas kernels  42.2 us (88%)
  local copies, waits for them, and re-layouts  4.67 us (10%)
  between operations  0.65 us (1%)
    pallas_call x1, Pallas kernels, solve_markets(): pl.pallas_call(market_kernel, out_shape=(jax.ShapeDtypeStruct((half, widt...  30.6 us
    pallas_call x1, Pallas kernels, route(): pl.pallas_call(functools.partial(route_kernel, markets), out_shape=jax.Sh...  9.67 us
    unnamed x3, local copies, waits for them, and re-layouts  4.67 us
    pallas_call x1, Pallas kernels, exchange(): pl.pallas_call(exchange_kernel, out_shape=jax.ShapeDtypeStruct((half,) +...  2.02 us

profile of v1, /device:TPU:0, one launch (start us, length us, event | category | flops | bytes accessed | tf_op | source)
XLA Modules:
  0.0 47.6 jit_solution(9743585213028388841)
XLA Ops:
  0.6 1.4 %copy.11.chars_ref = f32[8,6,128]{2,1,0:T(8,128)} copy(f32[8,6,128]{2,0,1:T(8,128)} %param.8) | data formatting | bytes 49152 | tf_op args[0]
  2.0 2.0 %copy.12.taste_ref = f32[8,6,2048]{2,1,0:T(8,128)} copy(f32[8,6,2048]{2,0,1:T(8,128)} %param.9) | data formatting | bytes 786432 | tf_op args[1]
  4.0 2.0 %exchange.1.other_ref = f32[4,6,2048]{2,1,0:T(8,128)} custom-call(f32[8,6,2048]{2,1,0:T(8,128)} %copy.12.taste_ref), custom_call_target="tpu_custom_call" | custom-call | tf_op jit(solution)/shard_map/exchange/pallas_call | solution.py:44
  6.0 30.6 %markets.1 = (f32[4,128]{1,0:T(4,128)}, f32[32,128]{1,0:T(8,128)}) custom-call(f32[6]{0:T(128)} %coef_ref.1, f32[2]{0:T(128)} %params_ref.1, s32[8]{0:T(128)} %bitcast.3, f32[8,6,128]{2,1,0:T(8,128)} %copy.11.chars_ref, f32[8,6,2048]{2,1,0:T(8,128)} %copy.12.taste_ref, f32[4,6,2048]{2,1,0:T(8,128)} %exchange.1.other_ref, f32[8,128]{1,0:T(8,128)} %prices_ref.1, ...), custom_call_target="tpu_custom_call" | custom-call | tf_op jit(solution)/shard_map/markets/pallas_call | solution.py:243
  36.6 9.7 %route.1 = f32[1,8,2,128]{3,2,1,0:T(2,128)} custom-call(f32[2,8,2,128]{3,2,1,0:T(2,128)} %bitcast.2), custom_call_target="tpu_custom_call" | custom-call | tf_op jit(solution)/shard_map/route/pallas_call | solution.py:302
  46.3 1.3 %copy.14 = f32[1,8,2,128]{3,2,1,0:T(2,128)} copy(f32[1,8,2,128]{3,2,1,0:T(2,128)} %route.1) | data formatting | bytes 16384

commit v2 on v1

--- a/solution.py
+++ b/solution.py
@@ -13,6 +13,10 @@
 LOG2E = 1.4426950408889634
 LN2 = 0.6931471805599453
 SWEEPS = 6
+U_SPREAD = 8
+U_FIRST = 32
+U_NEXT = 32
+U_LAST = 32
 DOUBLINGS = 26
 TOL = 3e-7
 MESH = pl.DeviceIdType.MESH
@@ -23,12 +27,11 @@
 
 def exchange_kernel(taste_ref, out_ref, send_sem, recv_sem):
     core = lax.axis_index("draw")
-    half = out_ref.shape[0]
     barrier = pltpu.get_barrier_semaphore()
     pl.semaphore_signal(barrier, inc=1, device_id={"draw": 1 - core}, device_id_type=MESH)
     pl.semaphore_wait(barrier, 1)
     copy = pltpu.make_async_remote_copy(
-        src_ref=taste_ref.at[pl.ds((1 - core) * half, half)],
+        src_ref=taste_ref,
         dst_ref=out_ref,
         send_sem=send_sem,
         recv_sem=recv_sem,
@@ -40,10 +43,9 @@
 
 
 def exchange(taste_draws):
-    half = taste_draws.shape[0] // 2
     return pl.pallas_call(
         exchange_kernel,
-        out_shape=jax.ShapeDtypeStruct((half,) + taste_draws.shape[1:], F32),
+        out_shape=jax.ShapeDtypeStruct(taste_draws.shape, F32),
         in_specs=[pl.BlockSpec(memory_space=pl.ANY)],
         out_specs=pl.BlockSpec(memory_space=pl.ANY),
         scratch_shapes=[pltpu.SemaphoreType.DMA, pltpu.SemaphoreType.DMA],
@@ -62,10 +64,11 @@
 def market_kernel(
     coef_ref, params_ref, steps_ref, chars_ref, taste_ref, other_ref, prices_ref, obs_ref,
     firms_ref, util_ref, placed_ref,
-    e_ref, q_ref, left_ref, right_ref, stack_ref, root_ref, v_ref, n_ref, m_ref,
+    e_ref, q_ref, left_ref, right_ref, stack_ref, root_ref, v_ref, n_ref, m_ref, b_ref, f_ref,
+    inv_ref,
 ):
     core = lax.axis_index("draw")
-    here, terms, width = chars_ref.shape
+    terms, here, width = chars_ref.shape
     half = here // 2
     part = taste_ref.shape[2]
     total = 2 * part
@@ -78,30 +81,35 @@
     eye = (row_i == col_i).astype(F32)
 
     obs_rows = [obs_ref[pl.ds(first + i, 1), :] for i in range(half)]
-    firm_rows = [firms_ref[pl.ds(first + i, 1), :].astype(F32) for i in range(half)]
     rows = jnp.zeros((width, width), F32)
     for i in range(half):
         rows = jnp.where(row_i == i, obs_rows[i], rows)
-        rows = jnp.where(row_i == half + i, firm_rows[i], rows)
+        firm_row = firms_ref[pl.ds(first + i, 1), :].astype(F32)
+        rows = jnp.where(row_i == half + i, firm_row, rows)
     cols = rows.T
-
-    finals = jnp.zeros((width, width), F32)
-    for i in range(half):
-        obs_row = obs_rows[i]
-        obs_col = cols[:, i:i + 1]
-        left_ref[...] = jnp.zeros_like(left_ref)
+    for i in range(half):
+        b_ref[i] = jnp.broadcast_to(cols[:, i:i + 1], (width, lanes))
+        f_ref[i] = jnp.broadcast_to(cols[:, half + i:half + i + 1], (width, lanes))
+    left_ref[...] = jnp.zeros_like(left_ref)
+    right_ref[...] = jnp.zeros_like(right_ref)
+
+    def market(i, finals):
+        m = first + i
+        obs_row = obs_ref[pl.ds(m, 1), :]
+        obs_col = b_ref[i]
         for k in range(terms):
-            left_ref[k:k + 1, :] = chars_ref[first + i, k:k + 1, :] * coef_ref[k] * LOG2E
-        left_ref[terms:terms + 1, :] = prices_ref[pl.ds(first + i, 1), :] * (-LOG2E)
+            left_ref[k:k + 1, :] = chars_ref[k, pl.ds(m, 1), :] * coef_ref[k] * LOG2E
+        left_ref[terms:terms + 1, :] = prices_ref[pl.ds(m, 1), :] * (-LOG2E)
         lh, lm, ll = split3(left_ref[...])
         left = jnp.concatenate([lh, lh, lm, lm, lh, ll], axis=0).T.astype(BF16)
-        right_ref[...] = jnp.zeros_like(right_ref)
-        for h in range(2):
-            taste = taste_ref[first + i] if h == 0 else other_ref[i]
-            log_sens = (params_ref[0] + params_ref[1] * taste[0:1, :]) * LOG2E
-            right_ref[0:terms, h * part:(h + 1) * part] = taste
-            right_ref[terms:terms + 1, h * part:(h + 1) * part] = jnp.exp2(log_sens)
-            root_ref[0:1, h * part:(h + 1) * part] = jnp.exp2(0.5 * log_sens)
+        for h, source in enumerate((taste_ref, other_ref)):
+            at = slice(h * part, (h + 1) * part)
+            for k in range(terms):
+                right_ref[k:k + 1, at] = source[k, pl.ds(m, 1), :]
+            log_sens = (params_ref[0] + params_ref[1] * right_ref[0:1, at]) * LOG2E
+            root = jnp.exp2(0.5 * log_sens)
+            root_ref[0:1, at] = root
+            right_ref[terms:terms + 1, at] = jnp.exp2(log_sens)
         xh, xm, xl = split3(right_ref[...])
         stack_ref[...] = jnp.concatenate([xh, xm, xh, xm, xl, xh], axis=0).astype(BF16)
 
@@ -116,12 +124,13 @@
             return top
 
         top = lax.fori_loop(
-            0, total // wide, spread_chunk, jnp.full((width, lanes), -jnp.inf, F32), unroll=2
+            0, total // wide, spread_chunk, jnp.full((width, lanes), -jnp.inf, F32),
+            unroll=U_SPREAD,
         )
         top = jnp.max(top, axis=1, keepdims=True)
         outside = 1.0 - jnp.sum(obs_row, axis=1, keepdims=True)
         start = (jnp.log(obs_col) - jnp.log(outside)) * LOG2E + top
-        v_ref[...] = jnp.broadcast_to(jnp.exp2(start), (width, lanes))
+        v_ref[...] = jnp.exp2(start)
         m_ref[...] = jnp.broadcast_to(top, (width, lanes))
 
         def first_chunk(c, acc):
@@ -137,15 +146,21 @@
             inv = 1.0 / (1.0 + jnp.sum(e * v_ref[...], axis=0, keepdims=True))
             return acc + e * inv
 
-        for turn in range(ITERS):
+        def evaluate(turn, share):
             acc = lax.fori_loop(
-                0, chunks, first_chunk if turn == 0 else next_chunk,
-                jnp.zeros((width, lanes), F32), unroll=4,
+                0, chunks, next_chunk, jnp.zeros((width, lanes), F32), unroll=U_NEXT
             )
             share = jnp.sum(acc, axis=1, keepdims=True) * (1.0 / total)
-            v_ref[...] = jnp.broadcast_to(obs_col / share, (width, lanes))
+            v_ref[...] = obs_col / share
+            return share
+
+        acc = lax.fori_loop(
+            0, chunks, first_chunk, jnp.zeros((width, lanes), F32), unroll=U_FIRST
+        )
+        share = jnp.sum(acc, axis=1, keepdims=True) * (1.0 / total)
+        v_ref[...] = obs_col / share
+        share = lax.fori_loop(1, ITERS, evaluate, share)
         mean = jnp.log(obs_col) - jnp.log(share) - top * LN2
-        finals = jnp.where(col_i == i, mean, finals)
 
         def last_chunk(c, acc):
             at = pl.ds(pl.multiple_of(c * lanes, lanes), lanes)
@@ -158,15 +173,17 @@
             q_ref[width:2 * width, at] = (q - high.astype(F32)).astype(BF16)
             return acc + q * root
 
-        own = lax.fori_loop(0, chunks, last_chunk, jnp.zeros((width, lanes), F32), unroll=4)
+        own = lax.fori_loop(0, chunks, last_chunk, jnp.zeros((width, lanes), F32), unroll=U_LAST)
         own = jnp.sum(own, axis=1, keepdims=True)
         both = lax.dot_general(
             q_ref[...], q_ref[...], (((1,), (1,)), ((), ())), preferred_element_type=F32
         )
         cross = both[0:width, 0:width] + (both[0:width, width:] + both[width:, 0:width])
-        same = cols[:, half + i:half + i + 1] == firm_rows[i]
+        same = f_ref[i] == firms_ref[pl.ds(m, 1), :].astype(F32)
         n_ref[i] = jnp.where(same, eye * own - cross, 0.0) * (1.0 / total)
-
+        return jnp.where(col_i == i, mean, finals)
+
+    finals = lax.fori_loop(0, half, market, jnp.zeros((width, width), F32))
     util_ref[...] = finals.T[0:half, :]
 
     scales, c_rows, c_cols, y_rows, y_cols = [], [], [], [], []
@@ -178,7 +195,7 @@
         n_ref[i] = eye - s_col * jac * s_row
         scales.append(s_row)
         c_rows.append(s_row * obs_rows[i])
-        c_cols.append(s_col * cols[:, i:i + 1])
+        c_cols.append(s_col * b_ref[i, :, 0:1])
     y_rows = tuple(c_rows)
 
     def sweep(_, ys):
@@ -234,7 +251,7 @@
 
 
 def solve_markets(coefs, params, steps, chars, taste, other, prices, obs, firms):
-    here, terms, width = chars.shape
+    terms, here, width = chars.shape
     half = here // 2
     total = 2 * taste.shape[2]
     smem = pl.BlockSpec(memory_space=pltpu.SMEM)
@@ -258,6 +275,9 @@
             pltpu.VMEM((width, 128), F32),
             pltpu.VMEM((half, width, width), F32),
             pltpu.VMEM((width, 128), F32),
+            pltpu.VMEM((half, width, 128), F32),
+            pltpu.VMEM((half, width, 128), F32),
+            pltpu.VMEM((8, total), F32),
         ],
         name="markets",
     )(coefs, params, steps, chars, taste, other, prices, obs, firms)
@@ -318,6 +338,8 @@
     markets,
     characters, taste_draws, prices, obs_shares, firm_ids, owner_step, spread_coefs, price_params,
 ):
+    characters = jnp.swapaxes(characters, 0, 1)
+    taste_draws = jnp.swapaxes(taste_draws, 0, 1)
     other = exchange(taste_draws)
     mean_util, placed = solve_markets(
         spread_coefs, price_params, owner_step[:, 0], characters, taste_draws, other,

time: 47.9 us -> 33 us (0.69)
  Pallas kernels: 42.2 us -> 30.8 us
  local copies, waits for them, and re-layouts: 4.67 us -> 1.3 us
    pallas_call x1, Pallas kernels: 30.6 us -> 18.8 us  [solve_markets(): pl.pallas_call(market_kernel, out_shape=(jax.ShapeDtypeStruct((half, widt...]
    unnamed x3 -> x1, local copies, waits for them, and re-layouts: 4.67 us -> 1.3 us
where the time goes in v2:
time: 33 us; the launch traced here: 32.7 us
  Pallas kernels  30.8 us (93%)
  local copies, waits for them, and re-layouts  1.3 us (4%)
  between operations  0.65 us (2%)
    pallas_call x1, Pallas kernels, solve_markets(): pl.pallas_call(market_kernel, out_shape=(jax.ShapeDtypeStruct((half, widt...  18.8 us
    pallas_call x1, Pallas kernels, route(): pl.pallas_call(functools.partial(route_kernel, markets), out_shape=jax.Sh...  9.71 us
    pallas_call x1, Pallas kernels, exchange(): pl.pallas_call(exchange_kernel, out_shape=jax.ShapeDtypeStruct(taste_draw...  2.24 us
    unnamed x1, local copies, waits for them, and re-layouts  1.3 us

profile of v2, /device:TPU:0, one launch (start us, length us, event | category | flops | bytes accessed | tf_op | source)
XLA Modules:
  0.0 32.7 jit_solution(13172685665012489400)
XLA Ops:
  0.6 2.2 %exchange.1.other_ref = f32[6,8,2048]{2,1,0:T(8,128)} custom-call(f32[6,8,2048]{2,1,0:T(8,128)} %bitcast.4), custom_call_target="tpu_custom_call" | custom-call | tf_op jit(solution)/shard_map/exchange/pallas_call | solution.py:46
  2.9 18.8 %markets.1 = (f32[4,128]{1,0:T(4,128)}, f32[32,128]{1,0:T(8,128)}) custom-call(f32[6]{0:T(128)} %coef_ref.1, f32[2]{0:T(128)} %params_ref.1, s32[8]{0:T(128)} %bitcast.8, f32[6,8,128]{2,1,0:T(8,128)} %bitcast.6, f32[6,8,2048]{2,1,0:T(8,128)} %bitcast.5, f32[6,8,2048]{2,1,0:T(8,128)} %exchange.1.other_ref, f32[8,128]{1,0:T(8,128)} %prices_ref.1, ...), custom_call_target="tpu_custom_call" | custom-call | tf_op jit(solution)/shard_map/markets/pallas_call | solution.py:260
  21.7 9.7 %route.1 = f32[1,8,2,128]{3,2,1,0:T(2,128)} custom-call(f32[2,8,2,128]{3,2,1,0:T(2,128)} %bitcast.7), custom_call_target="tpu_custom_call" | custom-call | tf_op jit(solution)/shard_map/route/pallas_call | solution.py:322
  31.4 1.3 %copy.11 = f32[1,8,2,128]{3,2,1,0:T(2,128)} copy(f32[1,8,2,128]{3,2,1,0:T(2,128)} %route.1) | data formatting | bytes 16384

commit v3 on v2

--- a/solution.py
+++ b/solution.py
@@ -159,7 +159,8 @@
         )
         share = jnp.sum(acc, axis=1, keepdims=True) * (1.0 / total)
         v_ref[...] = obs_col / share
-        share = lax.fori_loop(1, ITERS, evaluate, share)
+        for turn in range(1, ITERS):
+            share = evaluate(turn, share)
         mean = jnp.log(obs_col) - jnp.log(share) - top * LN2
 
         def last_chunk(c, acc):
@@ -283,7 +284,7 @@
     )(coefs, params, steps, chars, taste, other, prices, obs, firms)
 
 
-def route_kernel(markets, placed_ref, out_ref, got_ref, send_sem, recv_sem):
+def route_kernel(markets, placed_ref, got_ref, send_sem, recv_sem):
     core = lax.axis_index("draw")
     me = lax.axis_index("mkt")
     pairs = [(w, flip) for w in range(W) for flip in range(2) if (w, flip) != (0, 0)]
@@ -295,6 +296,8 @@
 
     for w, flip in pairs:
         pl.semaphore_signal(barrier, inc=1, device_id=peer(-w, flip), device_id_type=MESH)
+    keep = pltpu.make_async_copy(placed_ref.at[core, 0], got_ref.at[0, 0], send_sem.at[0, 0])
+    keep.start()
     pl.semaphore_wait(barrier, len(pairs))
     copies = []
     for w, flip in pairs:
@@ -311,21 +314,18 @@
         copies.append(copy)
     for copy in copies:
         copy.wait()
-    out_ref[0, 0] = placed_ref[core, 0] + got_ref[1, 0]
-    for w in range(1, W):
-        out_ref[0, w] = got_ref[0, w] + got_ref[1, w]
+    keep.wait()
 
 
 def route(markets, placed):
     width = placed.shape[-1]
-    vmem = pl.BlockSpec(memory_space=pltpu.VMEM)
+    anywhere = pl.BlockSpec(memory_space=pl.ANY)
     return pl.pallas_call(
         functools.partial(route_kernel, markets),
-        out_shape=jax.ShapeDtypeStruct((1, W, CAPC, width), F32),
-        in_specs=[vmem],
-        out_specs=vmem,
+        out_shape=jax.ShapeDtypeStruct((2, W, CAPC, width), F32),
+        in_specs=[anywhere],
+        out_specs=anywhere,
         scratch_shapes=[
-            pltpu.VMEM((2, W, CAPC, width), F32),
             pltpu.SemaphoreType.DMA((2, W)),
             pltpu.SemaphoreType.DMA((2, W)),
         ],
@@ -345,7 +345,8 @@
         spread_coefs, price_params, owner_step[:, 0], characters, taste_draws, other,
         prices, obs_shares, firm_ids,
     )
-    return mean_util, route(markets, placed)
+    got = route(markets, placed)
+    return mean_util, (got[0] + got[1])[None]
 
 
 def solution(mesh):

time: 33 us -> 31.3 us (0.948)
  Pallas kernels: 30.8 us -> 29.2 us
  other arithmetic: 0 us -> 1.32 us
  local copies, waits for them, and re-layouts: 1.3 us -> 0 us
    add x0 -> x1, other arithmetic: none -> 1.32 us  [body(): return (mean_util, (got[0] + got[1])[None])]
    unnamed x1 -> x0, local copies, waits for them, and re-layouts: 1.3 us -> none
    pallas_call x1, Pallas kernels: 9.71 us -> 8.69 us  [route(): pl.pallas_call(functools.partial(route_kernel, markets), out_shape=jax.Sh...]
    pallas_call x1, Pallas kernels: 18.8 us -> 18.2 us  [solve_markets(): pl.pallas_call(market_kernel, out_shape=(jax.ShapeDtypeStruct((half, widt...]
where the time goes in v3:
time: 31.3 us; the launch traced here: 31.1 us
  Pallas kernels  29.2 us (93%)
  other arithmetic  1.32 us (4%)
  between operations  0.65 us (2%)
    pallas_call x1, Pallas kernels, solve_markets(): pl.pallas_call(market_kernel, out_shape=(jax.ShapeDtypeStruct((half, widt...  18.2 us
    pallas_call x1, Pallas kernels, route(): pl.pallas_call(functools.partial(route_kernel, markets), out_shape=jax.Sh...  8.69 us
    pallas_call x1, Pallas kernels, exchange(): pl.pallas_call(exchange_kernel, out_shape=jax.ShapeDtypeStruct(taste_draw...  2.24 us
    add x1, other arithmetic, body(): return (mean_util, (got[0] + got[1])[None])  1.32 us

profile of v3, /device:TPU:0, one launch (start us, length us, event | category | flops | bytes accessed | tf_op | source)
XLA Modules:
  0.0 31.1 jit_solution(6182811472002495064)
XLA Ops:
  0.6 2.2 %exchange.1.other_ref = f32[6,8,2048]{2,1,0:T(8,128)} custom-call(f32[6,8,2048]{2,1,0:T(8,128)} %bitcast.4), custom_call_target="tpu_custom_call" | custom-call | tf_op jit(solution)/shard_map/exchange/pallas_call | solution.py:46
  2.9 18.2 %markets.1 = (f32[4,128]{1,0:T(4,128)}, f32[32,128]{1,0:T(8,128)}) custom-call(f32[6]{0:T(128)} %coef_ref.1, f32[2]{0:T(128)} %params_ref.1, s32[8]{0:T(128)} %bitcast.8, f32[6,8,128]{2,1,0:T(8,128)} %bitcast.6, f32[6,8,2048]{2,1,0:T(8,128)} %bitcast.5, f32[6,8,2048]{2,1,0:T(8,128)} %exchange.1.other_ref, f32[8,128]{1,0:T(8,128)} %prices_ref.1, ...), custom_call_target="tpu_custom_call" | custom-call | tf_op jit(solution)/shard_map/markets/pallas_call | solution.py:261
  21.1 8.7 %route.1 = f32[2,8,2,128]{3,2,1,0:T(2,128)} custom-call(f32[2,8,2,128]{3,2,1,0:T(2,128)} %bitcast.7), custom_call_target="tpu_custom_call" | custom-call | tf_op jit(solution)/shard_map/route/pallas_call | solution.py:323
  29.8 1.3 %slice_add_fusion = f32[1,8,2,128]{3,2,1,0:T(2,128)} fusion(f32[2,8,2,128]{3,2,1,0:T(2,128)} %route.1), kind=kLoop, calls=%fused_computation | loop fusion | flops 2048 | bytes 24576 | tf_op jit(solution)/shard_map/add | solution.py:349
